TPU v7x, 8 devices: a whole 2x2x1 slice. The times are simulated.
8 devices in a mesh: dp: 1 (over z), pool: 2 (over y), ep: 4 (over x, core).
Axes of the slice: x: 2, y: 2, z: 1, core: 2. Of those that a mesh axis runs over, the one named last changes fastest.
Arguments:
- hidden_in: bfloat16 [512, 896], P(('dp', 'ep'))
- k_cache: bfloat16 [2, 512, 512, 2, 128], P(None, ('dp', 'ep'), 'pool')
- v_cache: bfloat16 [2, 512, 512, 2, 128], P(None, ('dp', 'ep'), 'pool')
- cache_len: int32 [512], P(('dp', 'ep'))
- w_q: bfloat16 [2, 896, 2048], replicated
- w_k: bfloat16 [2, 896, 256], replicated
- w_v: bfloat16 [2, 896, 256], replicated
- w_o: bfloat16 [2, 2048, 896], replicated
- w_router: float32 [2, 896, 256], replicated
- expert_ids: int32 [2, 512, 8], P(None, ('dp', 'ep'))
- w_one: bfloat16 [2, 256, 896, 256], P(None, 'ep', None, 'pool')
- w_three: bfloat16 [2, 256, 896, 256], P(None, 'ep', None, 'pool')
- w_two: bfloat16 [2, 256, 256, 896], P(None, 'ep', 'pool')
Outputs:
- output: bfloat16 [512, 896], P(('dp', 'ep'))
All inputs are finite; a program needn't handle non-finite values.
Results may differ from a plain program's by a relative error of at most 0.02.
Values are sent between devices in bfloat16 or wider.
A program may use at most 1 GiB of HBM per device.

v0:
```python
import jax
import jax.numpy as jnp
from jax import lax
from jax.sharding import PartitionSpec as P

NORM_EPS = 1e-6


def rms_norm(in_vals):
    in_vals = in_vals.astype(jnp.float32)
    return in_vals * lax.rsqrt(jnp.mean(in_vals * in_vals, axis=-1, keepdims=True) + NORM_EPS)


def attention_block(hidden, k_rows, v_rows, cache_len, w_q, w_k, w_v, w_o):
    tokens = hidden.shape[0]
    seq_local, kv_heads, head_dim = k_rows.shape[1], k_rows.shape[2], k_rows.shape[3]
    n_heads = w_q.shape[1] // head_dim
    q_group = n_heads // kv_heads
    att_scale = head_dim ** -0.5
    normed = rms_norm(hidden).astype(jnp.bfloat16)
    query = jnp.dot(normed, w_q, preferred_element_type=jnp.float32).astype(jnp.bfloat16).reshape(tokens, kv_heads, q_group, head_dim)
    key_new = jnp.dot(normed, w_k, preferred_element_type=jnp.float32).astype(jnp.bfloat16).reshape(tokens, kv_heads, head_dim)
    val_new = jnp.dot(normed, w_v, preferred_element_type=jnp.float32).astype(jnp.bfloat16).reshape(tokens, kv_heads, head_dim)
    score_vals = jnp.einsum('tgqd,tsgd->tgqs', query, k_rows, preferred_element_type=jnp.float32) * att_scale
    positions = lax.axis_index('pool') * seq_local + jnp.arange(seq_local)
    pos_mask = positions[None, :] < cache_len[:, None]
    score_vals = jnp.where(pos_mask[:, None, None, :], score_vals, -1e30)
    new_score = jnp.einsum('tgqd,tgd->tgq', query, key_new, preferred_element_type=jnp.float32) * att_scale
    top_score = jnp.maximum(lax.pmax(jnp.max(score_vals, axis=-1), 'pool'), new_score)
    prob_vals = jnp.exp(score_vals - top_score[..., None])
    new_prob = jnp.exp(new_score - top_score)
    denom_sum = lax.psum(jnp.sum(prob_vals, axis=-1), 'pool') + new_prob
    numer_sum = lax.psum(jnp.einsum('tgqs,tsgd->tgqd', prob_vals.astype(jnp.bfloat16), v_rows, preferred_element_type=jnp.float32), 'pool')
    numer_sum = numer_sum + new_prob[..., None] * val_new.astype(jnp.float32)[:, :, None, :]
    attn_out = (numer_sum / denom_sum[..., None]).astype(jnp.bfloat16).reshape(tokens, n_heads * head_dim)
    return (hidden.astype(jnp.float32) + jnp.dot(attn_out, w_o, preferred_element_type=jnp.float32)).astype(jnp.bfloat16)


def router_gates(resid_rows, w_router, ids_layer):
    normed = rms_norm(resid_rows).astype(jnp.bfloat16)
    logits = jnp.dot(normed.astype(jnp.float32), w_router, preferred_element_type=jnp.float32)
    gate_vals = jax.nn.softmax(jnp.take_along_axis(logits, ids_layer, axis=1), axis=-1)
    return normed, gate_vals


def expert_math(tok_rows, group_sizes, w_one, w_three, w_two):
    h_one = lax.ragged_dot(tok_rows, w_one, group_sizes, preferred_element_type=jnp.float32)
    h_three = lax.ragged_dot(tok_rows, w_three, group_sizes, preferred_element_type=jnp.float32)
    act_rows = (jax.nn.silu(h_one) * h_three).astype(jnp.bfloat16)
    part_out = lax.ragged_dot(act_rows, w_two, group_sizes, preferred_element_type=jnp.float32)
    return lax.psum(part_out, 'pool').astype(jnp.bfloat16)


def local_experts(recv_rows, recv_ids, w_one, w_three, w_two):
    n_local = w_one.shape[0]
    sort_order = jnp.argsort(recv_ids, stable=True)
    group_sizes = jnp.bincount(recv_ids, length=n_local).astype(jnp.int32)
    sorted_rows = jnp.take(recv_rows, sort_order, axis=0)
    expert_out = expert_math(sorted_rows, group_sizes, w_one, w_three, w_two)
    return jnp.take(expert_out, jnp.argsort(sort_order), axis=0)


def solution(mesh):
    n_dev = mesh.shape['ep']
    tok_spec = P(('dp', 'ep'), None)
    cache_spec = P(None, ('dp', 'ep'), 'pool', None, None)
    up_spec = P(None, 'ep', None, 'pool')
    down_spec = P(None, 'ep', 'pool', None)
    in_specs = (tok_spec, cache_spec, cache_spec, P(('dp', 'ep')), P(), P(), P(), P(), P(), P(None, ('dp', 'ep'), None), up_spec, up_spec, down_spec)

    def body(hidden_in, k_cache, v_cache, cache_len, w_q, w_k, w_v, w_o, w_router, expert_ids, w_one, w_three, w_two):
        hidden = hidden_in
        n_local = w_one.shape[1]
        for layer_idx in range(w_q.shape[0]):
            ids_layer = expert_ids[layer_idx]
            tokens, top_k = ids_layer.shape
            resid_rows = attention_block(hidden, k_cache[layer_idx], v_cache[layer_idx], cache_len, w_q[layer_idx], w_k[layer_idx], w_v[layer_idx], w_o[layer_idx])
            normed, gate_vals = router_gates(resid_rows, w_router[layer_idx], ids_layer)
            flat_ids = ids_layer.reshape(-1)
            send_order = jnp.argsort(flat_ids // n_local, stable=True)
            pair_pos = jnp.argsort(send_order)
            send_rows = jnp.take(normed, send_order // top_k, axis=0)
            send_ids = jnp.take(flat_ids % n_local, send_order)
            recv_rows = lax.all_to_all(send_rows, 'ep', 0, 0, tiled=True)
            recv_ids = lax.all_to_all(send_ids, 'ep', 0, 0, tiled=True)
            expert_rows = local_experts(recv_rows, recv_ids, w_one[layer_idx], w_three[layer_idx], w_two[layer_idx])
            back_rows = lax.all_to_all(expert_rows, 'ep', 0, 0, tiled=True)
            pair_rows = jnp.take(back_rows, pair_pos, axis=0).reshape(tokens, top_k, -1)
            mixed_sum = jnp.sum(gate_vals[..., None] * pair_rows.astype(jnp.float32), axis=1)
            hidden = (resid_rows.astype(jnp.float32) + mixed_sum).astype(jnp.bfloat16)
        return hidden

    return jax.shard_map(body, mesh=mesh, in_specs=in_specs, out_specs=tok_spec, check_vma=False)
```

profile of v0, /device:TPU:0, one launch (start us, length us, event | category | flops | bytes accessed | tf_op | source)
XLA Modules:
  0.0 891.8 jit_solution(5076600236295633266)
XLA Ops:
  10.7 26.1 %fusion.126 = (bf16[1,128,256,2,128]{4,3,2,1,0:T(2,128)(2,1)}, bf16[1,128,256,2,128]{4,3,2,1,0:T(2,128)(2,1)}) fusion(bf16[2,128,256,2,128]{4,3,2,1,0:T(2,128)(2,1)} %param.22), kind=kLoop, calls=%fused_computation.217 | loop fusion | bytes 67108864 | tf_op jit(solution)/shard_map/slice | solution.py:77
  36.9 8.3 fusion.24
  45.2 11.7 %pmax.14 = f32[128,2,8]{2,1,0:T(2,128)S(1)} all-reduce(f32[128,2,8]{2,1,0:T(2,128)S(1)} %get-tuple-element.75), channel_id=1, replica_groups=mesh['dp'=1,'pool'=2,'ep'=4] {'pool'}, use_global_device_ids=true, to_apply=%region_2.3 | all-reduce | flops 2048 | bytes 16384 | tf_op jit(solution)/shard_map/pmax | solution.py:29
  58.7 26.1 %fusion.127 = (bf16[1,128,256,2,128]{4,3,2,1,0:T(2,128)(2,1)}, bf16[1,128,256,2,128]{4,3,2,1,0:T(2,128)(2,1)}) fusion(bf16[2,128,256,2,128]{4,3,2,1,0:T(2,128)(2,1)} %param.23), kind=kLoop, calls=%fused_computation.218 | loop fusion | bytes 67108864 | tf_op jit(solution)/shard_map/slice | solution.py:77
  84.9 9.2 %fusion.2 = f32[128,2,8,128]{3,2,1,0:T(8,128)} fusion(bf16[1,128,256,2,128]{4,3,2,1,0:T(2,128)(2,1)} %get-tuple-element.58, f32[128,2,8,256]{3,2,1,0:T(8,128)S(1)} %get-tuple-element.76, f32[128,2,8]{2,1,0:T(2,128)S(1)} %multiply_maximum_fusion.1, pred[128,256]{1,0:T(8,128)(4,1)S(1)} %broadcast_compare_fusion), kind=kOutput, calls=%fused_computation.19 | convolution fusion | flops 136314880 | bytes 19963904 | tf_op jit(solution)/shard_map/tgqs,tsgd->tgqd/dot_general | solution.py:33
  108.7 27.8 %slice_bitcast_fusion.2 = (bf16[64,896,128]{2,1,0:T(8,128)(2,1)}, bf16[64,896,128]{2,1,0:T(8,128)(2,1)}) fusion(bf16[2,64,896,128]{3,2,1,0:T(8,128)(2,1)} %param.31), kind=kLoop, calls=%fused_computation.24 | loop fusion | bytes 58720256 | tf_op jit(solution)/shard_map/squeeze | solution.py:86
  136.5 27.0 %slice_bitcast_fusion.1 = (bf16[64,896,128]{2,1,0:T(8,128)(2,1)}, bf16[64,896,128]{2,1,0:T(8,128)(2,1)}) fusion(bf16[2,64,896,128]{3,2,1,0:T(8,128)(2,1)} %param.32), kind=kLoop, calls=%fused_computation.23 | loop fusion | bytes 58720256 | tf_op jit(solution)/shard_map/squeeze | solution.py:86
  163.5 12.2 %slice_bitcast_fusion = (bf16[64,128,896]{2,1,0:T(8,128)(2,1)}, bf16[64,128,896]{2,1,0:T(8,128)(2,1)}) fusion(bf16[2,64,128,896]{3,2,1,0:T(8,128)(2,1)S(1)} %bitcast.173), kind=kLoop, calls=%fused_computation.22 | loop fusion | bytes 58720256 | tf_op jit(solution)/shard_map/squeeze | solution.py:86
  177.1 8.6 psum.43
  241.9 41.9 %ragged-dot-none.5 = f32[1024,128]{1,0:T(8,128)} custom-call(s32[1]{0:T(128)} %get-tuple-element.37, s32[65]{0:T(128)} %get-tuple-element.38, s32[67]{0:T(128)} %get-tuple-element.39, s32[67]{0:T(128)} %get-tuple-element.40, s32[1]{0:T(128)} %get-tuple-element.37, bf16[1024,896]{1,0:T(8,128)(2,1)} %broadcast_select_fusion.4, ...), custom_call_target="tpu_custom_call" | custom-call | flops 234881024 | bytes 17039616 | tf_op jit(solution)/shard_map/ragged_dot_general/ragged-dot-none
  283.8 42.0 %ragged-dot-none.4 = f32[1024,128]{1,0:T(8,128)} custom-call(s32[1]{0:T(128)} %get-tuple-element.37, s32[65]{0:T(128)} %get-tuple-element.38, s32[67]{0:T(128)} %get-tuple-element.39, s32[67]{0:T(128)} %get-tuple-element.40, s32[1]{0:T(128)} %get-tuple-element.37, bf16[1024,896]{1,0:T(8,128)(2,1)} %broadcast_select_fusion.4, ...), custom_call_target="tpu_custom_call" | custom-call | flops 234881024 | bytes 17039616 | tf_op jit(solution)/shard_map/ragged_dot_general/ragged-dot-none
  327.7 42.4 %ragged-dot-none.3 = f32[1024,896]{1,0:T(8,128)} custom-call(s32[1]{0:T(128)} %get-tuple-element.37, s32[65]{0:T(128)} %get-tuple-element.38, s32[67]{0:T(128)} %get-tuple-element.39, s32[67]{0:T(128)} %get-tuple-element.40, s32[1]{0:T(128)} %get-tuple-element.37, bf16[1024,128]{1,0:T(8,128)(2,1)} %multiply_convert_fusion.1, ...), custom_call_target="tpu_custom_call" | custom-call | flops 234881024 | bytes 18612480 | tf_op jit(solution)/shard_map/ragged_dot_general/ragged-dot-none
  370.1 90.5 %all-reduce.8 = bf16[1024,896]{1,0:T(8,128)(2,1)S(1)} all-reduce(f32[1024,896]{1,0:T(8,128)} %ragged-dot-none.3), channel_id=1, replica_groups=mesh['dp'=1,'pool'=2,'ep'=4] {'pool'}, use_global_device_ids=true, to_apply=%region_12.17 | all-reduce | flops 917504 | bytes 5505024 | tf_op jit(solution)/shard_map/psum | solution.py:51
  474.5 8.6 gather_fusion
  483.6 11.5 %all-to-all-done.2 = bf16[4,256,896]{2,1,0:T(8,128)(2,1)S(1)} async-done(((bf16[4,256,896]{2,1,0:T(8,128)(2,1)}), bf16[4,256,896]{2,1,0:T(8,128)(2,1)S(1)}, u32[]{:S(2)}, u32[]{:S(2)}) %all-to-all-start.2) | async-done | bytes 1835040 | tf_op jit(solution)/shard_map/all_to_all | solution.py:87
  518.7 8.5 pmax.15
  527.3 9.1 %fusion = f32[128,2,8,128]{3,2,1,0:T(8,128)} fusion(bf16[1,128,256,2,128]{4,3,2,1,0:T(2,128)(2,1)} %get-tuple-element.57, f32[128,2,8,256]{3,2,1,0:T(8,128)S(1)} %get-tuple-element.80, f32[128,2,8]{2,1,0:T(2,128)S(1)} %multiply_maximum_fusion, pred[128,256]{1,0:T(8,128)(4,1)S(1)} %broadcast_compare_fusion), kind=kOutput, calls=%fused_computation.15 | convolution fusion | flops 136314880 | bytes 19963904 | tf_op jit(solution)/shard_map/tgqs,tsgd->tgqd/dot_general | solution.py:33
  539.0 13.5 %psum.46 = f32[128,2,8]{2,1,0:T(2,128)S(1)} all-reduce(f32[128,2,8]{2,1,0:T(2,128)S(1)} %fusion.28), channel_id=1, replica_groups=mesh['dp'=1,'pool'=2,'ep'=4] {'pool'}, use_global_device_ids=true, to_apply=%region_21.26 | all-reduce | flops 2048 | bytes 16384 | tf_op jit(solution)/shard_map/psum | solution.py:32
  552.7 22.5 %all-reduce.7.cloned.1.call-done = f32[128,2,8,128]{3,2,1,0:T(8,128)} async-done(((f32[128,2,8,128]{3,2,1,0:T(8,128)}), f32[128,2,8,128]{3,2,1,0:T(8,128)}) %all-reduce.7.cloned.1.call-update) | async-done | bytes 1048592 | tf_op jit(solution)/shard_map/psum | solution.py:33
  620.1 43.9 %ragged-dot-none.2 = f32[1024,128]{1,0:T(8,128)} custom-call(s32[1]{0:T(128)} %get-tuple-element.25, s32[65]{0:T(128)} %get-tuple-element.26, s32[67]{0:T(128)} %get-tuple-element.27, s32[67]{0:T(128)} %get-tuple-element.28, s32[1]{0:T(128)} %get-tuple-element.25, bf16[1024,896]{1,0:T(8,128)(2,1)} %broadcast_select_fusion.1, ...), custom_call_target="tpu_custom_call" | custom-call | flops 234881024 | bytes 17039616 | tf_op jit(solution)/shard_map/ragged_dot_general/ragged-dot-none
  663.9 43.9 %ragged-dot-none.1 = f32[1024,128]{1,0:T(8,128)} custom-call(s32[1]{0:T(128)} %get-tuple-element.25, s32[65]{0:T(128)} %get-tuple-element.26, s32[67]{0:T(128)} %get-tuple-element.27, s32[67]{0:T(128)} %get-tuple-element.28, s32[1]{0:T(128)} %get-tuple-element.25, bf16[1024,896]{1,0:T(8,128)(2,1)} %broadcast_select_fusion.1, ...), custom_call_target="tpu_custom_call" | custom-call | flops 234881024 | bytes 17039616 | tf_op jit(solution)/shard_map/ragged_dot_general/ragged-dot-none
  709.7 44.3 %ragged-dot-none = f32[1024,896]{1,0:T(8,128)} custom-call(s32[1]{0:T(128)} %get-tuple-element.25, s32[65]{0:T(128)} %get-tuple-element.26, s32[67]{0:T(128)} %get-tuple-element.27, s32[67]{0:T(128)} %get-tuple-element.28, s32[1]{0:T(128)} %get-tuple-element.25, bf16[1024,128]{1,0:T(8,128)(2,1)} %multiply_convert_fusion, bf16[64,128,896]{2,1,0:T(8,128)(2,1)} %get-tuple-element.59), custom_call_target="tpu_custom_call" | custom-call | flops 234881024 | bytes 18612480 | tf_op jit(solution)/shard_map/ragged_dot_general/ragged-dot-none
  754.0 87.1 %all-reduce.9 = bf16[1024,896]{1,0:T(8,128)(2,1)S(1)} all-reduce(f32[1024,896]{1,0:T(8,128)} %ragged-dot-none), channel_id=1, replica_groups=mesh['dp'=1,'pool'=2,'ep'=4] {'pool'}, use_global_device_ids=true, to_apply=%region_28.33 | all-reduce | flops 917504 | bytes 5505024 | tf_op jit(solution)/shard_map/psum | solution.py:51
  859.0 8.6 gather_fusion.6
  (161 shorter events, 202.0 us)
Async XLA Ops:
  6.5 179.4 %all-reduce.5.cloned.1.call-start = ((), (), s32[]{:S(2)}) async-start(), calls=%async_computation.6 | async-start | bytes 2097152 | tf_op jit(solution)/shard_map/psum | solution.py:33
  10.7 26.1 %copy-start.4 = (s32[128]{0:T(128)S(1)}, s32[128]{0:T(128)}, u32[]{:S(2)}) copy-start(s32[128]{0:T(128)} %param.24) | copy-start | bytes 1540
  36.9 20.0 %copy-start.2 = (bf16[128,896]{1,0:T(8,128)(2,1)S(1)}, bf16[128,896]{1,0:T(8,128)(2,1)}, u32[]{:S(2)}) copy-start(bf16[128,896]{1,0:T(8,128)(2,1)} %param.21) | copy-start | bytes 688132
  84.8 9.3 %copy-start.3 = (s32[2,128,8]{1,2,0:T(8,128)S(1)}, s32[2,128,8]{1,2,0:T(8,128)}, u32[]{:S(2)}) copy-start(s32[2,128,8]{1,2,0:T(8,128)} %param.30) | copy-start | bytes 24580
  103.8 92.4 %all-to-all-start.1 = ((s32[4,256,1]{1,2,0:T(1,128)}), s32[4,256,1]{1,2,0:T(1,128)S(1)}, u32[]{:S(2)}, u32[]{:S(2)}) async-start(s32[4,256,1]{1,2,0:T(1,128)} %bitcast.11), calls=%async_computation.1 | async-start | bytes 8192 | tf_op jit(solution)/shard_map/all_to_all | solution.py:85
  108.7 54.8 %slice-start = ((s8[29360128]{0:T(1024)(128)(4,1)}), s8[4194304]{0:T(1024)(128)(4,1)S(1)}, s32[]{:S(2)}) async-start(s8[29360128]{0:T(1024)(128)(4,1)} %bitcast.172), calls=%async_computation.8 | async-start | bytes 8388608
  108.7 54.8 %slice-start.1 = ((s8[29360128]{0:T(1024)(128)(4,1)}), s8[4194304]{0:T(1024)(128)(4,1)S(1)}, s32[]{:S(2)}) async-start(s8[29360128]{0:T(1024)(128)(4,1)} %bitcast.172), calls=%async_computation.9 | async-start | bytes 8388608
  108.7 54.8 %slice-start.2 = ((s8[29360128]{0:T(1024)(128)(4,1)}), s8[4194304]{0:T(1024)(128)(4,1)S(1)}, s32[]{:S(2)}) async-start(s8[29360128]{0:T(1024)(128)(4,1)} %bitcast.172), calls=%async_computation.10 | async-start | bytes 8388608
  108.7 54.8 %slice-start.3 = ((s8[29360128]{0:T(1024)(128)(4,1)}), s8[4194304]{0:T(1024)(128)(4,1)S(1)}, s32[]{:S(2)}) async-start(s8[29360128]{0:T(1024)(128)(4,1)} %bitcast.172), calls=%async_computation.11 | async-start | bytes 8388608
  136.5 27.0 %slice-start.4 = ((s8[29360128]{0:T(1024)(128)(4,1)}), s8[4194304]{0:T(1024)(128)(4,1)S(1)}, s32[]{:S(2)}) async-start(s8[29360128]{0:T(1024)(128)(4,1)} %bitcast.172), calls=%async_computation.12 | async-start | bytes 8388608
  136.5 27.0 %slice-start.5 = ((s8[29360128]{0:T(1024)(128)(4,1)}), s8[4194304]{0:T(1024)(128)(4,1)S(1)}, s32[]{:S(2)}) async-start(s8[29360128]{0:T(1024)(128)(4,1)} %bitcast.172), calls=%async_computation.13 | async-start | bytes 8388608
  136.5 27.0 %slice-start.6 = ((s8[29360128]{0:T(1024)(128)(4,1)}), s8[4194304]{0:T(1024)(128)(4,1)S(1)}, s32[]{:S(2)}) async-start(s8[29360128]{0:T(1024)(128)(4,1)} %bitcast.172), calls=%async_computation.14 | async-start | bytes 8388608
  196.2 37.4 %all-to-all-start = ((bf16[4,256,896]{2,1,0:T(8,128)(2,1)}), bf16[4,256,896]{2,1,0:T(8,128)(2,1)S(1)}, u32[]{:S(2)}, u32[]{:S(2)}) async-start(bf16[4,256,896]{2,1,0:T(8,128)(2,1)} %bitcast.174), calls=%async_computation | async-start | bytes 3670016 | tf_op jit(solution)/shard_map/all_to_all | solution.py:84
  283.8 42.0 %copy-start.1 = (f32[1024,128]{1,0:T(8,128)S(1)}, f32[1024,128]{1,0:T(8,128)}, u32[]{:S(2)}) copy-start(f32[1024,128]{1,0:T(8,128)} %ragged-dot-none.5) | copy-start | bytes 1572868
  468.9 26.2 %all-to-all-start.2 = ((bf16[4,256,896]{2,1,0:T(8,128)(2,1)}), bf16[4,256,896]{2,1,0:T(8,128)(2,1)S(1)}, u32[]{:S(2)}, u32[]{:S(2)}) async-start(bf16[4,256,896]{2,1,0:T(8,128)(2,1)} %bitcast.177), calls=%async_computation.2 | async-start | bytes 3670016 | tf_op jit(solution)/shard_map/all_to_all | solution.py:87
  495.1 90.5 %all-to-all-start.4 = ((s32[4,256,1]{1,2,0:T(1,128)}), s32[4,256,1]{1,2,0:T(1,128)S(1)}, u32[]{:S(2)}, u32[]{:S(2)}) async-start(s32[4,256,1]{1,2,0:T(1,128)} %bitcast.33), calls=%async_computation.4 | async-start | bytes 8192 | tf_op jit(solution)/shard_map/all_to_all | solution.py:85
  498.3 76.9 %all-reduce.7.cloned.1.call-start = ((), (), s32[]{:S(2)}) async-start(), calls=%async_computation.7 | async-start | bytes 2097152 | tf_op jit(solution)/shard_map/psum | solution.py:33
  503.6 3.1 copy-start.5
  585.6 26.2 %all-to-all-start.3 = ((bf16[4,256,896]{2,1,0:T(8,128)(2,1)}), bf16[4,256,896]{2,1,0:T(8,128)(2,1)S(1)}, u32[]{:S(2)}, u32[]{:S(2)}) async-start(bf16[4,256,896]{2,1,0:T(8,128)(2,1)} %bitcast.175), calls=%async_computation.3 | async-start | bytes 3670016 | tf_op jit(solution)/shard_map/all_to_all | solution.py:84
  663.9 43.9 %copy-start = (f32[1024,128]{1,0:T(8,128)S(1)}, f32[1024,128]{1,0:T(8,128)}, u32[]{:S(2)}) copy-start(f32[1024,128]{1,0:T(8,128)} %ragged-dot-none.2) | copy-start | bytes 1572868
  849.5 26.2 %all-to-all-start.5 = ((bf16[4,256,896]{2,1,0:T(8,128)(2,1)}), bf16[4,256,896]{2,1,0:T(8,128)(2,1)S(1)}, u32[]{:S(2)}, u32[]{:S(2)}) async-start(bf16[4,256,896]{2,1,0:T(8,128)(2,1)} %bitcast.176), calls=%async_computation.5 | async-start | bytes 3670016 | tf_op jit(solution)/shard_map/all_to_all | solution.py:87
Sparse Core Ops, SparseCore 0:
  94.2 34.1 all-reduce.4
  536.6 38.5 all-reduce.6
where the time goes:
time: 903 us; the launch traced here: 892 us
  Pallas kernels  265 us (29%)
  blocking collectives  220 us (24%)
  local copies, waits for them, and re-layouts  186 us (21%)
  other arithmetic  86.7 us (10%)
  matrix products  54.1 us (6%)
  waiting for transfers between devices  43.8 us (5%)
  starting transfers between devices  21 us (2%)
  between operations  14.6 us (2%)
    another operation x6, Pallas kernels  258 us
    psum x2, blocking collectives, expert_math(): return lax.psum(part_out, 'pool').astype(jnp.bfloat16)  178 us
    squeeze x1, local copies, waits for them, and re-layouts, body(): w_one[layer_idx]  27.8 us
    squeeze x1, local copies, waits for them, and re-layouts, body(): w_three[layer_idx]  27 us
    slice x1, local copies, waits for them, and re-layouts, body(): k_cache[layer_idx]  26.1 us
    slice x1, local copies, waits for them, and re-layouts, body(): v_cache[layer_idx]  26.1 us
    psum x2, waiting for transfers between devices, attention_block(): lax.psum(jnp.einsum('tgqs,tsgd->tgqd', prob_vals.astype(jnp.bfloat16), v_...  22.5 us
    psum x2, blocking collectives, attention_block(): denom_sum = lax.psum(jnp.sum(prob_vals, axis=-1), 'pool') + new_prob  22.1 us
  transfers between devices with their start and end apart: 8, of which 4 were waited for; matrix products, arithmetic and copies ran while one was open for 23% of the time, Pallas kernels for 1%

commit v1 on v0

v1 whole, which is shorter than its diff:
```python
import functools

import jax
import jax.numpy as jnp
from jax import lax
from jax.experimental import pallas as pl
from jax.experimental.pallas import tpu as pltpu
from jax.sharding import PartitionSpec as P

MESH = pl.DeviceIdType.MESH
F32, BF16, I32 = jnp.float32, jnp.bfloat16, jnp.int32
NORM_EPS = 1e-6
T, D, HD, H = 128, 896, 128, 16
HALF = T // 2
KV = 2
POS = 256
ROWS = POS * KV
CH = 8
NCH = T // CH
NB = 8
ALL = 4 * T
NE = 64
PAIRS = 1024
FF = 128
NW = 24
MC = 32
CM = 384
NX = 8
XR = PAIRS // NX
VMEM_LIMIT = 60 * 1024 * 1024


def rms(v):
    v = v.astype(F32)
    return v * lax.rsqrt(jnp.mean(v * v, axis=-1, keepdims=True) + NORM_EPS)


def mm(a, b):
    return jnp.dot(a, b, preferred_element_type=F32)


def iota(shape, dim):
    return lax.broadcasted_iota(I32, shape, dim)


def peers():
    g, p, e = lax.axis_index("dp"), lax.axis_index("pool"), lax.axis_index("ep")
    core = lax.rem(e, 2)
    e_x = lax.rem(e + 2, 4)
    e_d = e + 1 - 2 * core
    e_z = lax.rem(e_d + 2, 4)
    return p, e, e_x, e_d, e_z, (g, 1 - p, e), (g, p, e_x), (g, p, e_d), (g, p, e_z)


def entry_barrier(targets):
    bar = pltpu.get_barrier_semaphore()
    for dev in targets:
        pl.semaphore_signal(bar, inc=1, device_id=dev, device_id_type=MESH)
    pl.semaphore_wait(bar, len(targets))


def remote(src, dst, send_sem, recv_sem, dev):
    return pltpu.make_async_remote_copy(src_ref=src, dst_ref=dst, send_sem=send_sem, recv_sem=recv_sem,
                                        device_id=dev, device_id_type=MESH)


def attn_kernel(layer, first, *refs):
    if first:
        (x_ref, len_ref, idt_ref, k_ref, v_ref, wq_ref, wk_ref, wv_ref, wo_ref, a_ref, ida_ref, *scr) = refs
    else:
        (x_ref, len_ref, k_ref, v_ref, wq_ref, wk_ref, wv_ref, wo_ref, a_ref, *scr) = refs
    (kbuf, vbuf, wq_v, wk_v, wv_v, wo_v, q2d, kn2d, vn2d, num, nrec, stat, ssend, srec,
     kv_sem, w_sem, ns_sem, nr_sem, ss_sem, sr_sem, gs_sem, gr_sem, is_sem, ir_sem) = scr
    p, e, e_x, e_d, e_z, dev_y, dev_x, dev_d, dev_z = peers()

    def tok_of(c):
        first_half = (1 - p) * HALF + c * CH
        second_half = p * HALF + (c - NCH // 2) * CH
        return pl.multiple_of(jnp.where(c < NCH // 2, first_half, second_half), CH)

    def kv_copies(c):
        slot = lax.rem(c, NB)
        src = pl.ds(tok_of(c), CH)
        return (pltpu.make_async_copy(k_ref.at[layer, src], kbuf.at[slot], kv_sem.at[0, slot]),
                pltpu.make_async_copy(v_ref.at[layer, src], vbuf.at[slot], kv_sem.at[1, slot]))

    weights = [pltpu.make_async_copy(r.at[layer], b, w_sem.at[i])
               for i, (r, b) in enumerate(((wq_ref, wq_v), (wk_ref, wk_v), (wv_ref, wv_v), (wo_ref, wo_v)))]
    for cp in weights[:3]:
        cp.start()
    for c in range(NB):
        for cp in kv_copies(jnp.int32(c)):
            cp.start()
    weights[3].start()

    entry_barrier((dev_y, dev_x, dev_d, dev_z))

    id_copies = []
    if first:
        mine = (slice(None), slice(None), pl.ds(pl.multiple_of(e * T, T), T))
        ida_ref[mine] = idt_ref[...]
        for i, dev in enumerate((dev_x, dev_d, dev_z)):
            id_copies.append(remote(idt_ref, ida_ref.at[mine], is_sem.at[i], ir_sem.at[i], dev))
            id_copies[-1].start()

    normed = rms(x_ref[...]).astype(BF16)
    for cp in weights[:3]:
        cp.wait()
    for hp in range(H // 2):
        pair = mm(normed, wq_v[:, hp * 256:(hp + 1) * 256]).astype(BF16).astype(F32)
        for i in range(2):
            q2d[pl.ds(hp * 2 + i, T, stride=H), :] = pair[:, i * HD:(i + 1) * HD]
    for w, dst in ((wk_v, kn2d), (wv_v, vn2d)):
        pair = mm(normed, w[...]).astype(BF16).astype(F32)
        for i in range(KV):
            dst[pl.ds(i, T, stride=KV), :] = pair[:, i * HD:(i + 1) * HD]

    scale = HD ** -0.5
    col = iota((H, ROWS), 1)
    group_ok = (col & 1) == (iota((H, ROWS), 0) // (H // KV))
    col_pos = jnp.where(group_ok, col >> 1, 1 << 30)
    lane = iota((H, T), 1)

    def heads_of(ref, tok):
        two = ref[pl.ds(tok * KV, KV), :]
        return jnp.concatenate([jnp.broadcast_to(two[i:i + 1], (H // KV, HD)) for i in range(KV)], axis=0)

    def num_copy(c):
        rows = pl.ds(pl.multiple_of(c * (CH * H), CH * H), CH * H)
        return remote(num.at[rows], nrec.at[rows], ns_sem.at[c], nr_sem.at[c], dev_y)

    stat_copy = remote(ssend, srec, ss_sem, sr_sem, dev_y)

    def chunk(c, carry):
        slot = lax.rem(c, NB)
        for cp in kv_copies(c):
            cp.wait()
        tok0 = tok_of(c)
        m_all, l_all, n_all = stat[0], stat[1], stat[2]
        for j0 in range(0, CH, 4):
            group = range(j0, j0 + 4)
            qs, ss = {}, {}
            for j in group:
                qs[j] = q2d[pl.ds(pl.multiple_of((tok0 + j) * H, H), H), :]
                ss[j] = lax.dot_general(qs[j].astype(BF16), kbuf[slot, j], (((1,), (1,)), ((), ())),
                                        preferred_element_type=F32) * scale
            ps = {}
            for j in group:
                limit = len_ref[tok0 + j] - p * POS
                s = jnp.where(col_pos < limit, ss[j], -1e30)
                s_new = jnp.sum(qs[j] * heads_of(kn2d, tok0 + j), axis=1, keepdims=True) * scale
                m = jnp.maximum(jnp.max(s, axis=1, keepdims=True), s_new)
                pr = jnp.exp(s - m)
                ps[j] = pr.astype(BF16)
                here = lane == c * CH + j
                m_all = jnp.where(here, m, m_all)
                l_all = jnp.where(here, jnp.sum(pr, axis=1, keepdims=True), l_all)
                n_all = jnp.where(here, s_new, n_all)
            for j in group:
                num[pl.ds(pl.multiple_of((c * CH + j) * H, H), H), :] = mm(ps[j], vbuf[slot, j])
        stat[0], stat[1], stat[2] = m_all, l_all, n_all

        @pl.when(c + NB < NCH)
        def _():
            for cp in kv_copies(c + NB):
                cp.start()

        @pl.when(c == NCH // 2 - 1)
        def _():
            ssend[0], ssend[1] = m_all, l_all

        @pl.when((c >= 1) & (c <= NCH // 2))
        def _():
            num_copy(c - 1).start()

        @pl.when(c == NCH // 2)
        def _():
            stat_copy.start()

        return carry

    stat[...] = jnp.zeros_like(stat)
    lax.fori_loop(0, NCH, chunk, 0)

    weights[3].wait()
    stat_copy.wait()
    m_own, l_own, s_new = stat[0], stat[1], stat[2]
    m_far = pltpu.roll(srec[0], HALF, axis=1)
    l_far = pltpu.roll(srec[1], HALF, axis=1)
    m = jnp.maximum(m_own, m_far)
    w_own, w_far, w_new = jnp.exp(m_own - m), jnp.exp(m_far - m), jnp.exp(s_new - m)
    denom = l_own * w_own + l_far * w_far + w_new
    c_own, c_far, c_new = w_own / denom, w_far / denom, w_new / denom

    def combine(c, carry):
        num_copy(c).wait()
        for j in range(CH):
            i = c * CH + j
            pick = lane == HALF + i
            own, far, new = [jnp.sum(jnp.where(pick, v, 0.0), axis=1, keepdims=True) for v in (c_own, c_far, c_new)]
            there = pl.ds(pl.multiple_of(i * H, H), H)
            here = pl.ds(pl.multiple_of((HALF + i) * H, H), H)
            num[here, :] = num[here, :] * own + nrec[there, :] * far + heads_of(vn2d, p * HALF + i) * new
        return carry

    lax.fori_loop(0, NCH // 2, combine, 0)

    proj = jnp.zeros((HALF, D), F32)
    for hp in range(H // 2):
        pair = jnp.concatenate([num[pl.ds(HALF * H + hp * 2 + i, HALF, stride=H), :].astype(BF16) for i in range(2)], axis=1)
        proj = proj + mm(pair, wo_v[hp * 256:(hp + 1) * 256, :])
    mine = pl.ds(pl.multiple_of(p * HALF, HALF), HALF)

    def rows(pp, ee):
        return pl.ds(pl.multiple_of(ee * T + pp * HALF, HALF), HALF)

    a_ref[rows(p, e), :] = (x_ref[mine, :].astype(F32) + proj).astype(BF16)

    def gather(i, pp, ee, dev):
        block = a_ref.at[rows(pp, ee)]
        cp = remote(block, block, gs_sem.at[i], gr_sem.at[i], dev)
        cp.start()
        return cp

    copies = [gather(0, p, e, dev_y), gather(1, p, e, dev_x), gather(2, p, e, dev_d)]
    copies[0].wait_recv()
    copies += [gather(3, 1 - p, e, dev_x), gather(4, 1 - p, e, dev_d)]
    copies[1].wait_recv()
    copies += [gather(5, p, e_x, dev_d)]
    copies[3].wait_recv()
    copies += [gather(6, 1 - p, e_x, dev_d)]
    for i in (2, 4, 5, 6):
        copies[i].wait_recv()
    for cp in copies:
        cp.wait_send()
    for cp in id_copies:
        cp.wait()


def attention(layer, x, cache_len, id_t, k, v, wq, wk, wv, wo, cid):
    first = id_t is not None
    vm, sm, hb = (pl.BlockSpec(memory_space=m) for m in (pltpu.VMEM, pltpu.SMEM, pl.ANY))
    dma = pltpu.SemaphoreType.DMA
    outs = [jax.ShapeDtypeStruct((ALL, D), BF16)]
    if first:
        outs.append(jax.ShapeDtypeStruct((id_t.shape[0], 8, ALL), I32))
    out = pl.pallas_call(
        functools.partial(attn_kernel, layer, first),
        name=f"attn_{layer}",
        out_shape=outs,
        in_specs=[vm, sm] + ([vm] if first else []) + [hb] * 6,
        out_specs=[vm] * len(outs),
        scratch_shapes=[
            pltpu.VMEM((NB, CH, ROWS, HD), BF16), pltpu.VMEM((NB, CH, ROWS, HD), BF16),
            pltpu.VMEM((D, H * HD), BF16), pltpu.VMEM((D, KV * HD), BF16), pltpu.VMEM((D, KV * HD), BF16),
            pltpu.VMEM((H * HD, D), BF16),
            pltpu.VMEM((T * H, HD), F32), pltpu.VMEM((T * KV, HD), F32), pltpu.VMEM((T * KV, HD), F32),
            pltpu.VMEM((T * H, HD), F32), pltpu.VMEM((HALF * H, HD), F32),
            pltpu.VMEM((3, H, T), F32), pltpu.VMEM((2, H, T), F32), pltpu.VMEM((2, H, T), F32),
            dma((2, NB)), dma((4,)), dma((NCH // 2,)), dma((NCH // 2,)), dma(()), dma(()),
            dma((7,)), dma((7,)), dma((3,)), dma((3,)),
        ],
        compiler_params=pltpu.CompilerParams(collective_id=cid, has_side_effects=True, vmem_limit_bytes=VMEM_LIMIT),
    )(*([x, cache_len] + ([id_t] if first else []) + [k, v, wq, wk, wv, wo]))
    return out if first else (out[0], None)


def expert_kernel(layer, a_ref, idt_ref, w1_ref, w3_ref, w2_ref, ym_ref, yt_ref,
                  w1b, w3b, w2b, u, xs, ym, yt, tail, pos, meta, smeta, w_sem, m_sem, o_sem):
    e = lax.axis_index("ep")

    def w_copies(i):
        slot = lax.rem(i, NW)
        return [pltpu.make_async_copy(r.at[layer, i], b.at[slot], w_sem.at[n, slot])
                for n, (r, b) in enumerate(((w1_ref, w1b), (w3_ref, w3b), (w2_ref, w2b)))]

    def start(i, carry):
        for cp in w_copies(i):
            cp.start()
        return carry

    lax.fori_loop(0, NW, start, 0)

    u[...] = rms(a_ref[...]).astype(BF16)
    sub = iota((128, ALL), 0)
    local = [idt_ref[layer, k:k + 1, :] - e * NE for k in range(8)]
    local = [jnp.where((v >= 0) & (v < NE), v, -1) for v in local]
    mask = jnp.zeros((128, ALL), F32)
    for v in local:
        mask = jnp.where(v == sub, 1.0, mask)
    mask_b = mask.astype(BF16)
    before = (iota((ALL, ALL), 0) < iota((ALL, ALL), 1)).astype(BF16)
    rank = mm(mask_b, before)
    n_col = jnp.broadcast_to(jnp.sum(mask, axis=1, keepdims=True), (128, 128)).astype(I32)
    n_row = lax.dot_general(jnp.ones((8, ALL), BF16), mask_b, (((1,), (1,)), ((), ())),
                            preferred_element_type=F32).astype(I32)
    lower = (iota((128, 128), 1) < iota((128, 128), 0)).astype(BF16)
    upper = (iota((128, 128), 0) < iota((128, 128), 1)).astype(BF16)
    as_b = lambda v: v.astype(F32).astype(BF16)
    off_col = mm(lower, as_b((n_col + 15) >> 4)) * 16.0
    off_row = mm(as_b((n_row + 15) >> 4), upper)
    offc_row = mm(as_b(n_row >> 4), upper) * 16.0 + mm(as_b(n_row & 15), upper)
    meta[0] = n_row
    meta[1] = off_row.astype(I32)
    meta[2] = offc_row.astype(I32)
    m_copy = pltpu.make_async_copy(meta, smeta, m_sem)
    m_copy.start()
    where_to = off_col[:, 0:1] + rank + 1.0
    for k in range(8):
        pos[k:k + 1, :] = (jnp.sum(jnp.where(local[k] == sub, where_to, 0.0), axis=0, keepdims=True) - 1.0).astype(I32)
    m_copy.wait()

    def dispatch(i, carry):
        row = iota((256, ALL), 0) + i * 256
        hit = jnp.zeros((256, ALL), F32)
        for k in range(8):
            hit = jnp.where(pos[k:k + 1, :] == row, 1.0, hit)
        xs[pl.ds(pl.multiple_of(i * 256, 256), 256), :] = mm(hit.astype(BF16), u[...]).astype(BF16)
        return carry

    lax.fori_loop(0, (smeta[1, 0, NE] + 15) >> 4, dispatch, 0)

    def expert(i, carry):
        slot = lax.rem(i, NW)
        for cp in w_copies(i):
            cp.wait()
        n, off, offc = smeta[0, 0, i], smeta[1, 0, i], smeta[2, 0, i]

        def rows_step(j, c2):
            rows = xs[pl.ds(pl.multiple_of(off * 16 + j * MC, 16), MC), :]
            act = (jax.nn.silu(mm(rows, w1b[slot])) * mm(rows, w3b[slot])).astype(BF16)
            y = mm(act, w2b[slot])
            to = pl.ds(offc + j * MC, MC)
            for t in range(6):
                ym[t // 3, t % 3, to, :] = y[:, t * 128:(t + 1) * 128]
            yt[to, :] = y[:, 2 * CM:]
            return c2

        lax.fori_loop(0, (n + MC - 1) // MC, rows_step, 0)

        @pl.when(i + NW < NE)
        def _():
            start(i + NW, 0)

        return carry

    lax.fori_loop(0, NE, expert, 0)
    out = pltpu.make_async_copy(ym.at[:, :, pl.ds(0, PAIRS)], ym_ref, o_sem.at[0])
    out.start()
    top, bot = yt[:PAIRS // 2, :], yt[PAIRS // 2:PAIRS, :]
    left = iota((PAIRS // 2, 128), 1) < 64
    tail[0] = jnp.where(left, top, pltpu.roll(bot, 64, axis=1))
    tail[1] = jnp.where(left, pltpu.roll(top, 64, axis=1), bot)
    out2 = pltpu.make_async_copy(tail, yt_ref, o_sem.at[1])
    out2.start()
    out.wait()
    out2.wait()


def experts(layer, a_all, id_t, w1, w3, w2):
    vm, hb = (pl.BlockSpec(memory_space=m) for m in (pltpu.VMEM, pl.ANY))
    dma = pltpu.SemaphoreType.DMA
    return pl.pallas_call(
        functools.partial(expert_kernel, layer),
        name=f"experts_{layer}",
        out_shape=[jax.ShapeDtypeStruct((2, 3, PAIRS, 128), F32), jax.ShapeDtypeStruct((2, PAIRS // 2, 128), F32)],
        in_specs=[vm, vm, hb, hb, hb],
        out_specs=[hb, hb],
        scratch_shapes=[
            pltpu.VMEM((NW, D, FF), BF16), pltpu.VMEM((NW, D, FF), BF16), pltpu.VMEM((NW, FF, D), BF16),
            pltpu.VMEM((ALL, D), BF16), pltpu.VMEM((2304, D), BF16),
            pltpu.VMEM((2, 3, PAIRS + MC, 128), F32), pltpu.VMEM((PAIRS + MC, 128), F32),
            pltpu.VMEM((2, PAIRS // 2, 128), F32),
            pltpu.VMEM((8, ALL), I32), pltpu.VMEM((3, 8, 128), I32), pltpu.SMEM((3, 8, 128), I32),
            dma((3, NW)), dma(()), dma((2,)),
        ],
        compiler_params=pltpu.CompilerParams(vmem_limit_bytes=VMEM_LIMIT),
    )(a_all, id_t, w1, w3, w2)


def merge_kernel(layer, a_ref, id_ref, ym_ref, yt_ref, wr_ref, x_ref,
                 my_m, my_t, rec_m, rec_t, wr, gate, acc_m, acc_t, back_m, back_t, send_m, send_t, far_m, far_t,
                 l_sem, xs_sem, xr_sem, bs_sem, br_sem, fs_sem, fr_sem):
    p, e, e_x, e_d, e_z, dev_y, dev_x, dev_d, dev_z = peers()
    loads = [pltpu.make_async_copy(src, dst, l_sem.at[i])
             for i, (src, dst) in enumerate(((wr_ref.at[layer], wr), (ym_ref.at[p], my_m), (yt_ref.at[p], my_t)))]
    for cp in loads:
        cp.start()
    entry_barrier((dev_y, dev_x, dev_d, dev_z))

    def y_copy(c):
        block = pl.ds(c * XR, XR)
        return remote(ym_ref.at[1 - p, :, block], rec_m.at[:, block], xs_sem.at[c], xr_sem.at[c], dev_y)

    t_copy = remote(yt_ref.at[1 - p], rec_t, xs_sem.at[NX], xr_sem.at[NX], dev_y)
    y_copies = [y_copy(c) for c in range(NX)]
    for cp in y_copies:
        cp.start()
    t_copy.start()

    loads[0].wait()
    u = rms(a_ref[...]).astype(BF16)
    logits = jnp.zeros((ALL, 256), F32)
    rest = wr[...]
    for _ in range(3):
        part = rest.astype(BF16)
        rest = rest - part.astype(F32)
        logits = logits + mm(u, part)
    col = iota((ALL, 256), 1)
    ids = [id_ref[layer, :, k:k + 1] for k in range(8)]
    g = [jnp.sum(jnp.where(v == col, logits, 0.0), axis=1, keepdims=True) for v in ids]
    top = functools.reduce(jnp.maximum, g)
    g = [jnp.exp(v - top) for v in g]
    total = functools.reduce(jnp.add, g)
    g = [v / total for v in g]

    lane = iota((ALL, 128), 1)
    local = [jnp.where((v >= e * NE) & (v < (e + 1) * NE), v - e * NE, -1) for v in ids]
    mask = jnp.zeros((ALL, 128), F32)
    for v in local:
        mask = jnp.where(v == lane, 1.0, mask)
    mask_b = mask.astype(BF16)
    before = (iota((ALL, ALL), 1) < iota((ALL, ALL), 0)).astype(BF16)
    rank = mm(before, mask_b)
    n_row = mm(jnp.ones((8, ALL), BF16), mask_b).astype(I32)
    upper = (iota((128, 128), 0) < iota((128, 128), 1)).astype(BF16)
    as_b = lambda v: v.astype(F32).astype(BF16)
    offc = mm(as_b(n_row >> 4), upper) * 16.0 + mm(as_b(n_row & 15), upper)
    where_to = offc[0:1, :] + rank + 1.0
    pos = [(jnp.sum(jnp.where(v == lane, where_to, 0.0), axis=1, keepdims=True) - 1.0).astype(I32) for v in local]

    for c in range(PAIRS // 128):
        w = jnp.zeros((ALL, 128), F32)
        for k in range(8):
            w = jnp.where(pos[k] == lane + c * 128, g[k], w)
        for i in range(3):
            part = w.astype(BF16)
            w = w - part.astype(F32)
            gate[i, :, c * 128:(c + 1) * 128] = part

    def mix(block, y):
        return sum(mm(gate[i, :, block], y) for i in range(3))

    loads[1].wait()
    loads[2].wait()
    for c in range(NX):
        block = slice(c * XR, (c + 1) * XR)
        y_copies[c].wait_recv()
        part = mix(block, jnp.concatenate([(my_m[t, block, :] + rec_m[t, block, :]).astype(BF16) for t in range(3)], axis=1))
        acc_m[...] = part if c == 0 else acc_m[...] + part
    t_copy.wait_recv()
    y_tail = (my_t[...] + rec_t[...]).astype(BF16)
    half0, half1 = mix(slice(0, PAIRS // 2), y_tail), mix(slice(PAIRS // 2, PAIRS), y_tail)
    keep0 = jnp.broadcast_to(p == 0, half0.shape)
    acc_t[...] = jnp.where(keep0, half0, pltpu.roll(half0, 64, axis=1)) + jnp.where(keep0, pltpu.roll(half1, 64, axis=1), half1)

    def block_of(ee):
        return pl.ds(pl.multiple_of(ee * T, T), T)

    backs = []
    for i, (ee, dev) in enumerate(((e_x, dev_x), (e_z, dev_z), (e_d, dev_d))):
        backs.append(remote(acc_m.at[block_of(ee)], back_m.at[i], bs_sem.at[2 * i], br_sem.at[2 * i], dev))
        backs.append(remote(acc_t.at[block_of(ee)], back_t.at[i], bs_sem.at[2 * i + 1], br_sem.at[2 * i + 1], dev))
    for cp in backs:
        cp.start()
    sum_m, sum_t = acc_m[block_of(e), :], acc_t[block_of(e), :]
    a_m = a_ref[block_of(e), pl.ds(pl.multiple_of(p * CM, CM), CM)].astype(F32)
    a_t = a_ref[block_of(e), 2 * CM:].astype(F32)
    for i in (2, 0, 1):
        backs[2 * i].wait_recv()
        backs[2 * i + 1].wait_recv()
        sum_m = sum_m + back_m[i]
        sum_t = sum_t + back_t[i]
    send_m[...] = (a_m + sum_m).astype(BF16)
    send_t[...] = (a_t + sum_t).astype(BF16)
    outs = [remote(send_m, far_m, fs_sem.at[0], fr_sem.at[0], dev_y),
            remote(send_t, far_t, fs_sem.at[1], fr_sem.at[1], dev_y)]
    for cp in outs:
        cp.start()
    x_ref[:, pl.ds(pl.multiple_of(p * CM, CM), CM)] = send_m[...]
    for cp in outs:
        cp.wait()
    x_ref[:, pl.ds(pl.multiple_of((1 - p) * CM, CM), CM)] = far_m[...]
    keep_own = (iota((T, 128), 1) // 64) == p
    x_ref[:, 2 * CM:] = jnp.where(keep_own, send_t[...].astype(F32), far_t[...].astype(F32)).astype(BF16)
    for cp in y_copies + [t_copy] + backs:
        cp.wait_send()


def merge(layer, a_all, ids, ym, yt, wr, cid):
    vm, hb = (pl.BlockSpec(memory_space=m) for m in (pltpu.VMEM, pl.ANY))
    dma = pltpu.SemaphoreType.DMA
    return pl.pallas_call(
        functools.partial(merge_kernel, layer),
        name=f"merge_{layer}",
        out_shape=jax.ShapeDtypeStruct((T, D), BF16),
        in_specs=[vm, vm, hb, hb, hb],
        out_specs=vm,
        scratch_shapes=[
            pltpu.VMEM((3, PAIRS, 128), F32), pltpu.VMEM((PAIRS // 2, 128), F32),
            pltpu.VMEM((3, PAIRS, 128), F32), pltpu.VMEM((PAIRS // 2, 128), F32),
            pltpu.VMEM((D, 256), F32), pltpu.VMEM((3, ALL, PAIRS), BF16),
            pltpu.VMEM((ALL, CM), F32), pltpu.VMEM((ALL, 128), F32),
            pltpu.VMEM((3, T, CM), F32), pltpu.VMEM((3, T, 128), F32),
            pltpu.VMEM((T, CM), BF16), pltpu.VMEM((T, 128), BF16),
            pltpu.VMEM((T, CM), BF16), pltpu.VMEM((T, 128), BF16),
            dma((3,)), dma((NX + 1,)), dma((NX + 1,)), dma((6,)), dma((6,)), dma((2,)), dma((2,)),
        ],
        compiler_params=pltpu.CompilerParams(collective_id=cid, has_side_effects=True, vmem_limit_bytes=VMEM_LIMIT),
    )(a_all, ids, ym, yt, wr)


def solution(mesh):
    tok_spec = P(('dp', 'ep'), None)
    cache_spec = P(None, ('dp', 'ep'), 'pool', None, None)
    up_spec = P(None, 'ep', None, 'pool')
    down_spec = P(None, 'ep', 'pool', None)
    in_specs = (tok_spec, cache_spec, cache_spec, P(('dp', 'ep')), P(), P(), P(), P(), P(), P(None, ('dp', 'ep'), None),
                up_spec, up_spec, down_spec)

    def body(hidden, k_cache, v_cache, cache_len, w_q, w_k, w_v, w_o, w_router, expert_ids, w_one, w_three, w_two):
        layers = w_q.shape[0]
        k = k_cache.reshape(layers, T, ROWS, HD)
        v = v_cache.reshape(layers, T, ROWS, HD)
        id_t = jnp.swapaxes(expert_ids, 1, 2)
        ids_t = ids = None
        for layer in range(layers):
            a_all, gathered = attention(layer, hidden, cache_len, id_t if layer == 0 else None, k, v, w_q, w_k, w_v, w_o, 2 * layer)
            if layer == 0:
                ids_t, ids = gathered, jnp.swapaxes(gathered, 1, 2)
            ym, yt = experts(layer, a_all, ids_t, w_one, w_three, w_two)
            hidden = merge(layer, a_all, ids, ym, yt, w_router, 2 * layer + 1)
        return hidden

    return jax.shard_map(body, mesh=mesh, in_specs=in_specs, out_specs=tok_spec, check_vma=False)
```

time: 903 us -> 275 us (0.30); the launches traced: 892 us -> 275 us
  blocking collectives: 220 us -> 0 us
  local copies, waits for them, and re-layouts: 186 us -> 3.39 us
  other arithmetic: 86.7 us -> 0 us
  matrix products: 54.1 us -> 0 us
  waiting for transfers between devices: 43.8 us -> 0 us
  starting transfers between devices: 21 us -> 0 us
  between operations: 14.6 us -> 0.05 us
    pallas_call x0 -> x6, Pallas kernels: none -> 271 us  [the longest x2 126 us: merge(): pl.pallas_call(functools.partial(merge_kernel, layer), name=f'merge_{laye...]
    another operation x6 -> x0, Pallas kernels: 258 us -> none
    psum x4 -> x0, blocking collectives: 200 us -> none  [the longest x2 178 us: expert_math(): return lax.psum(part_out, 'pool').astype(jnp.bfloat16)]
    squeeze x3 -> x0, local copies, waits for them, and re-layouts: 66.9 us -> none  [the longest x1 27.8 us: body(): w_one[layer_idx]]
    gather x16 -> x0, local copies, waits for them, and re-layouts: 66.2 us -> none  [the longest x6 17.5 us: router_gates(): jnp.take_along_axis(logits, ids_layer, axis=1)]
    dot_general x16 -> x0, matrix products: 54.1 us -> none  [the longest x2 18.4 us: attention_block(): jnp.einsum('tgqs,tsgd->tgqd', prob_vals.astype(jnp.bfloat16), v_rows, pre...]
    slice x3 -> x0, local copies, waits for them, and re-layouts: 52.2 us -> none  [the longest x1 26.1 us: body(): k_cache[layer_idx]]
    sort x8 -> x0, other arithmetic: 34.9 us -> none  [the longest x2 8.73 us: local_experts(): return jnp.take(expert_out, jnp.argsort(sort_order), axis=0)]
  transfers between devices with their start and end apart: 8 -> 0, of which waited for: 4 -> 0; matrix products, arithmetic and copies ran while one was open for 23% -> 0% of each run, Pallas kernels for 1% -> 0%
where the time goes in v1:
time: 275 us
  Pallas kernels  271 us (99%)
  local copies, waits for them, and re-layouts  3.39 us (1%)
    pallas_call x2, Pallas kernels, merge(): pl.pallas_call(functools.partial(merge_kernel, layer), name=f'merge_{laye...  126 us
    pallas_call x2, Pallas kernels, attention(): pl.pallas_call(functools.partial(attn_kernel, layer, first), name=f'attn_...  73.9 us
    pallas_call x2, Pallas kernels, experts(): pl.pallas_call(functools.partial(expert_kernel, layer), name=f'experts_{l...  71.1 us

profile of v1, /device:TPU:0, one launch (start us, length us, event | category | flops | bytes accessed | tf_op | source)
XLA Modules:
  0.0 274.6 jit_solution(9275390253259952488)
XLA Ops:
  0.0 37.6 %attn_0.1 = (bf16[512,896]{1,0:T(8,128)(2,1)}, s32[2,8,512]{2,1,0:T(8,128)}) custom-call(bf16[128,896]{1,0:T(8,128)(2,1)} %refs_0_.1, s32[128]{0:T(128)} %refs_1_.3, s32[2,8,128]{2,1,0:T(8,128)} %bitcast.10, bf16[2,128,512,128]{3,2,1,0:T(8,128)(2,1)} %bitcast.4, bf16[2,128,512,128]{3,2,1,0:T(8,128)(2,1)} %bitcast.6, bf16[2,896,2048]{2,1,0:T(8,128)(2,1)} %refs_4_.1, ...), custom_call_target="tpu_custom_call" | custom-call | tf_op jit(solution)/shard_map/attn_0/pallas_call | solution.py:247
  37.6 1.7 copy.14
  39.4 34.5 %experts_0.1 = (f32[2,3,1024,128]{3,2,1,0:T(8,128)}, f32[2,512,128]{2,1,0:T(8,128)}) custom-call(bf16[512,896]{1,0:T(8,128)(2,1)} %get-tuple-element.11.a_ref, s32[2,8,512]{2,1,0:T(8,128)} %get-tuple-element.12.idt_ref, bf16[2,64,896,128]{3,2,1,0:T(8,128)(2,1)} %w1_ref.3, bf16[2,64,896,128]{3,2,1,0:T(8,128)(2,1)} %w3_ref.3, bf16[2,64,128,896]{3,2,1,0:T(8,128)(2,1)} %w2_ref.3), custom_call_target="tpu_custom_call" | custom-call | tf_op jit(solution)/shard_map/experts_0/pallas_call | solution.py:363
  73.9 63.0 %merge_0.1.refs_0_ = bf16[128,896]{1,0:T(8,128)(2,1)} custom-call(bf16[512,896]{1,0:T(8,128)(2,1)} %get-tuple-element.11.a_ref, s32[2,512,8]{2,1,0:T(8,128)} %bitcast.8, f32[2,3,1024,128]{3,2,1,0:T(8,128)} %get-tuple-element.13.ym_ref, f32[2,512,128]{2,1,0:T(8,128)} %get-tuple-element.14.yt_ref, f32[2,896,256]{2,1,0:T(8,128)} %wr_ref.3), custom_call_target="tpu_custom_call" | custom-call | tf_op jit(solution)/shard_map/merge_0/pallas_call | solution.py:493
  136.9 36.3 %attn_1.1.a_ref = bf16[512,896]{1,0:T(8,128)(2,1)} custom-call(bf16[128,896]{1,0:T(8,128)(2,1)} %merge_0.1.refs_0_, s32[128]{0:T(128)} %refs_1_.3, bf16[2,128,512,128]{3,2,1,0:T(8,128)(2,1)} %bitcast.5, bf16[2,128,512,128]{3,2,1,0:T(8,128)(2,1)} %bitcast.7, bf16[2,896,2048]{2,1,0:T(8,128)(2,1)} %refs_4_.1, bf16[2,896,256]{2,1,0:T(8,128)(2,1)} %refs_5_.3, ...), custom_call_target="tpu_custom_call" | custom-call | tf_op jit(solution)/shard_map/attn_1/pallas_call | solution.py:247
  173.2 36.6 %experts_1.1 = (f32[2,3,1024,128]{3,2,1,0:T(8,128)}, f32[2,512,128]{2,1,0:T(8,128)}) custom-call(bf16[512,896]{1,0:T(8,128)(2,1)} %attn_1.1.a_ref, s32[2,8,512]{2,1,0:T(8,128)} %get-tuple-element.12.idt_ref, bf16[2,64,896,128]{3,2,1,0:T(8,128)(2,1)} %w1_ref.3, bf16[2,64,896,128]{3,2,1,0:T(8,128)(2,1)} %w3_ref.3, bf16[2,64,128,896]{3,2,1,0:T(8,128)(2,1)} %w2_ref.3), custom_call_target="tpu_custom_call" | custom-call | tf_op jit(solution)/shard_map/experts_1/pallas_call | solution.py:363
  209.8 63.1 %merge_1.1 = bf16[128,896]{1,0:T(8,128)(2,1)} custom-call(bf16[512,896]{1,0:T(8,128)(2,1)} %attn_1.1.a_ref, s32[2,512,8]{2,1,0:T(8,128)} %bitcast.9, f32[2,3,1024,128]{3,2,1,0:T(8,128)} %get-tuple-element.15.ym_ref, f32[2,512,128]{2,1,0:T(8,128)} %get-tuple-element.16.yt_ref, f32[2,896,256]{2,1,0:T(8,128)} %wr_ref.3), custom_call_target="tpu_custom_call" | custom-call | tf_op jit(solution)/shard_map/merge_1/pallas_call | solution.py:493
  272.9 1.6 copy.16
